TPU v7x, 8 devices: a whole 2x2x1 slice. The times are simulated.
8 devices in a mesh: frag: 2 (over z, y), dev: 4 (over x, core).
Axes of the slice: x: 2, y: 2, z: 1, core: 2. Of those that a mesh axis runs over, the one named last changes fastest.
Arguments:
- a_ints: bfloat16 [192, 96, 96, 96], P(('frag', 'dev')), parts along dimension 0
- c_occ: bfloat16 [192, 20], P('frag'), parts along dimension 0
- c_vir: bfloat16 [192, 75], P('frag'), parts along dimension 0
- eps_occ: float32 [40], P('frag'), parts along dimension 0
- eps_vir: float32 [150], P('frag'), parts along dimension 0
Outputs:
- output: float32 [40, 20], P('frag', 'dev'), parts along dimension 0
There are 2 independent parts. A program takes and returns all parts, laid end to end along the dimension named above; each array names one.
All inputs are finite; a program needn't handle non-finite values.
Results may differ from a plain program's by a relative error of at most 0.001.
Values are sent between devices in bfloat16 or wider.
A program may use at most 1 GiB of HBM per device.

v0:
```python
import jax
import jax.numpy as jnp
from jax import lax
from jax.sharding import PartitionSpec as P, NamedSharding


def pair_energies(v_mo, eps_j, eps_occ, eps_vir):
    v_swap = jnp.swapaxes(v_mo, 1, 2)
    denominator = (eps_j[:, None, None, None] + eps_occ[None, None, None, :]
                   - eps_vir[None, :, None, None] - eps_vir[None, None, :, None])
    pair_ji = jnp.sum(v_mo * (2.0 * v_mo - v_swap) / denominator, axis=(1, 2))
    return pair_ji.T


def solution(mesh):
    group_size = mesh.shape["dev"]

    def per_device(a_ints, c_occ, c_vir, eps_occ, eps_vir):
        occ_dev = c_occ.shape[1] // group_size
        t_one = jnp.einsum("pqrs,rj->pqsj", a_ints, c_occ, preferred_element_type=jnp.float32).astype(jnp.bfloat16)
        half_mo = jnp.einsum("pqsj,sb->pqjb", t_one, c_vir, preferred_element_type=jnp.float32).astype(jnp.bfloat16)
        half_mo = lax.all_to_all(half_mo, "dev", 2, 0, tiled=True)
        g_mat = jnp.einsum("pqjb,qa->pjba", half_mo, c_vir, preferred_element_type=jnp.float32).astype(jnp.bfloat16)
        v_mo = jnp.einsum("pjba,pi->jbai", g_mat, c_occ, preferred_element_type=jnp.float32)
        eps_j = lax.dynamic_slice_in_dim(eps_occ, lax.axis_index("dev") * occ_dev, occ_dev)
        return pair_energies(v_mo, eps_j, eps_occ, eps_vir)

    return jax.shard_map(
        per_device,
        mesh=mesh,
        in_specs=(P(("frag", "dev")), P("frag"), P("frag"), P("frag"), P("frag")),
        out_specs=P("frag", "dev"),
        check_vma=False,
    )
```

profile of v0, /device:TPU:0, one launch (start us, length us, event | category | flops | bytes accessed | tf_op | source)
XLA Modules:
  0.0 203.5 jit_solution(11539995414660299104)
XLA Ops:
  0.0 0.0 copy-start
  0.0 25.6 %convolution_convert_fusion = bf16[24,96,96,20]{2,3,1,0:T(8,128)(2,1)} fusion(bf16[24,96,96,96]{3,2,1,0:T(8,128)(2,1)} %param.5, bf16[96,20]{0,1:T(8,128)(2,1)} %param.6), kind=kOutput, calls=%fused_computation.2 | convolution fusion | flops 853770240 | bytes 51318528 | tf_op jit(solution)/shard_map/pqrs,rj->pqsj/dot_general | solution.py:20
  25.6 0.0 copy-done
  25.6 17.4 %fusion.4 = bf16[24,96,20,75]{1,3,2,0:T(8,128)(2,1)} fusion(bf16[24,96,96,20]{2,3,1,0:T(8,128)(2,1)} %convolution_convert_fusion, bf16[96,75]{0,1:T(8,128)(2,1)S(1)} %copy-done), kind=kOutput, calls=%fused_computation.5 | convolution fusion | flops 667008000 | bytes 15773760 | tf_op jit(solution)/shard_map/pqsj,sb->pqjb/dot_general | solution.py:21
  43.0 13.4 %copy.13 = bf16[24,96,20,75]{1,0,3,2:T(8,128)(2,1)} copy(bf16[24,96,20,75]{1,3,2,0:T(8,128)(2,1)} %fusion.4) | data formatting | bytes 13824000 | tf_op jit(solution)/shard_map/convert_element_type | solution.py:21
  56.4 0.0 copy-start.3
  56.4 0.0 copy-start.2
  56.4 6.1 %all-to-all-start = ((bf16[24,96,20,75]{1,0,3,2:T(8,128)(2,1)}), bf16[24,96,20,75]{1,0,3,2:T(8,128)(2,1)}, u32[]{:S(2)}, u32[]{:S(2)}) async-start(bf16[24,96,20,75]{1,0,3,2:T(8,128)(2,1)} %copy.13), calls=%async_computation | async-start | bytes 18432000 | tf_op jit(solution)/shard_map/all_to_all | solution.py:22
  62.5 0.0 copy-done.3
  62.5 0.1 dynamic_slice.3
  62.6 0.1 broadcast_add_fusion
  62.7 0.0 copy-done.2
  62.7 0.1 broadcast_subtract_fusion
  62.7 102.5 %all-to-all-done = bf16[24,96,20,75]{1,0,3,2:T(8,128)(2,1)} async-done(((bf16[24,96,20,75]{1,0,3,2:T(8,128)(2,1)}), bf16[24,96,20,75]{1,0,3,2:T(8,128)(2,1)}, u32[]{:S(2)}, u32[]{:S(2)}) %all-to-all-start) | async-done | bytes 6912032 | tf_op jit(solution)/shard_map/all_to_all | solution.py:22
  165.3 0.0 copy-start.1
  165.3 8.8 %copy.14 = bf16[4,24,96,5,75]{2,1,0,4,3:T(8,128)(2,1)} copy(bf16[4,24,96,5,75]{2,1,4,3,0:T(8,128)(2,1)} %bitcast.5) | data formatting | bytes 13824000 | tf_op jit(solution)/shard_map/all_to_all | solution.py:22
  174.0 0.0 copy-done.1
  174.0 17.6 %fusion.2 = f32[5,75,75,20]{2,3,1,0:T(8,128)} fusion(bf16[96,96,5,75]{1,0,3,2:T(8,128)(2,1)} %bitcast.30, bf16[96,75]{0,1:T(8,128)(2,1)S(1)} %copy-done, bf16[96,20]{0,1:T(8,128)(2,1)S(1)} %copy-done.1), kind=kOutput, calls=%fused_computation.3 | convolution fusion | flops 629100032 | bytes 9180240 | tf_op jit(solution)/shard_map/pjba,pi->jbai/dot_general | solution.py:24
  191.7 6.3 %copy.15 = f32[5,75,75,20]{1,3,2,0:T(8,128)} copy(f32[5,75,75,20]{2,3,1,0:T(8,128)} %fusion.2) | data formatting | bytes 4500000 | tf_op jit(solution)/shard_map/pjba,pi->jbai/dot_general | solution.py:24
  197.9 5.5 %fusion.11 = f32[5,20]{1,0:T(8,128)} fusion(f32[5,75,75,20]{2,3,1,0:T(8,128)} %fusion.2, f32[5,75,75,20]{1,3,2,0:T(8,128)} %copy.15, f32[75]{0:T(128)S(1)} %copy-done.2, f32[5,75,20]{2,1,0:T(8,128)S(1)} %broadcast_subtract_fusion), kind=kLoop, calls=%fused_computation.10 | loop fusion | flops 3374900 | bytes 4530700 | tf_op jit(solution)/shard_map/reduce_sum | solution.py:11
Async XLA Ops:
  0.0 25.6 %copy-start = (bf16[96,75]{0,1:T(8,128)(2,1)S(1)}, bf16[96,75]{0,1:T(8,128)(2,1)}, u32[]{:S(2)}) copy-start(bf16[96,75]{0,1:T(8,128)(2,1)} %param.7) | copy-start | bytes 43204
  56.4 6.1 %copy-start.3 = (f32[20]{0:T(128)S(1)}, f32[20]{0:T(128)}, u32[]{:S(2)}) copy-start(f32[20]{0:T(128)} %param.8) | copy-start | bytes 244
  56.4 6.3 %copy-start.2 = (f32[75]{0:T(128)S(1)}, f32[75]{0:T(128)}, u32[]{:S(2)}) copy-start(f32[75]{0:T(128)} %param.9) | copy-start | bytes 904
  56.4 108.9 %all-to-all-start = ((bf16[24,96,20,75]{1,0,3,2:T(8,128)(2,1)}), bf16[24,96,20,75]{1,0,3,2:T(8,128)(2,1)}, u32[]{:S(2)}, u32[]{:S(2)}) async-start(bf16[24,96,20,75]{1,0,3,2:T(8,128)(2,1)} %copy.13), calls=%async_computation | async-start | bytes 18432000 | tf_op jit(solution)/shard_map/all_to_all | solution.py:22
  165.3 8.8 %copy-start.1 = (bf16[96,20]{0,1:T(8,128)(2,1)S(1)}, bf16[96,20]{0,1:T(8,128)(2,1)}, u32[]{:S(2)}) copy-start(bf16[96,20]{0,1:T(8,128)(2,1)} %param.6) | copy-start | bytes 11524
where the time goes:
time: 204 us; the launch traced here: 203 us
  waiting for transfers between devices  103 us (50%)
  matrix products  60.6 us (30%)
  local copies, waits for them, and re-layouts  28.5 us (14%)
  starting transfers between devices  6.12 us (3%)
  other arithmetic  5.7 us (3%)
    all_to_all x1, waiting for transfers between devices, per_device(): half_mo = lax.all_to_all(half_mo, 'dev', 2, 0, tiled=True)  103 us
    dot_general x1, matrix products, per_device(): jnp.einsum('pqrs,rj->pqsj', a_ints, c_occ, preferred_element_type=jnp.flo...  25.6 us
    dot_general x1, matrix products, per_device(): jnp.einsum('pjba,pi->jbai', g_mat, c_occ, preferred_element_type=jnp.floa...  17.6 us
    dot_general x1, matrix products, per_device(): jnp.einsum('pqsj,sb->pqjb', t_one, c_vir, preferred_element_type=jnp.floa...  17.4 us
    convert_element_type x1, local copies, waits for them, and re-layouts, per_device(): jnp.einsum('pqsj,sb->pqjb', t_one, c_vir, preferred_element_type=jnp.floa...  13.4 us
    all_to_all x1, local copies, waits for them, and re-layouts, per_device(): half_mo = lax.all_to_all(half_mo, 'dev', 2, 0, tiled=True)  8.76 us
    dot_general x1, local copies, waits for them, and re-layouts, per_device(): jnp.einsum('pjba,pi->jbai', g_mat, c_occ, preferred_element_type=jnp.floa...  6.28 us
    all_to_all x1, starting transfers between devices, per_device(): half_mo = lax.all_to_all(half_mo, 'dev', 2, 0, tiled=True)  6.12 us
  transfers between devices with their start and end apart: 1, of which 1 were waited for; matrix products, arithmetic and copies ran while one was open for 0% of the time, Pallas kernels for 0%

commit v1 on v0

v1 whole, which is shorter than its diff:
```python
import functools

import jax
import jax.numpy as jnp
from jax import lax
from jax.experimental import pallas as pl
from jax.experimental.pallas import tpu as pltpu
from jax.sharding import PartitionSpec as P

MESH = pl.DeviceIdType.MESH
F32, BF16 = jnp.float32, jnp.bfloat16

N = 96
O = 20
V = 75
NDEV = 4
NP = N // NDEV
OD = O // NDEV
L = 128
JB = 384
PC = 4
NC = NP // PC
AQ = 19
GR = AQ * 4 * PC
SLOTS = 3


def _dot(x, y):
    return jnp.dot(x, y, preferred_element_type=F32)


def _div(x, d):
    return jnp.floor((x + 0.5) * (1.0 / d))


def _rows(shape):
    return lax.broadcasted_iota(jnp.int32, shape, 0).astype(F32)


def _cols(shape):
    return lax.broadcasted_iota(jnp.int32, shape, 1).astype(F32)


def _onehot(cond):
    return jnp.where(cond, 1.0, 0.0).astype(BF16)


def _spread(m, row_of, col_of, keep, shape):
    r_shape, c_shape = (shape[0], m.shape[0]), (m.shape[1], shape[1])
    left = _onehot(row_of(_rows(r_shape)) == _cols(r_shape))
    right = _onehot(_rows(c_shape) == col_of(_cols(c_shape)))
    full = _dot(_dot(left, m).astype(BF16), right)
    return jnp.where(keep(_rows(shape), _cols(shape)), full, 0.0).astype(BF16)


def kernel(a_hbm, co_ref, cv_ref, eo_ref, ev_ref, out_ref, a_buf, l1, w2, l3, l4, t_s, h_s, g_send, g_recv,
           v_s, r_s, e_s, a_sem, send_sem, recv_sem):
    f, me = lax.axis_index("frag"), lax.axis_index("dev")
    chip, core = me // 2, lax.rem(me, 2)
    far0 = (1 - chip) * 2 + core
    far1 = (1 - chip) * 2 + 1 - core
    near = chip * 2 + 1 - core
    peers = (far0, far1, near)

    def a_copy(p, slot):
        return pltpu.make_async_copy(a_hbm.at[p], a_buf.at[slot], a_sem.at[slot])

    for s in range(SLOTS):
        a_copy(s, s).start()

    barrier = pltpu.get_barrier_semaphore()
    for d in peers:
        pl.semaphore_signal(barrier, inc=1, device_id=(f, d), device_id_type=MESH)

    co, cv = co_ref[...], cv_ref[...]
    mod = lambda x, d: x - d * _div(x, d)
    l1[...] = _spread(co, lambda x: mod(x, O), lambda y: mod(y, N), lambda x, y: _div(x, O) == _div(y, N), (2 * O, 2 * N))
    cv_t = cv.astype(F32).T.astype(BF16)
    for jj in range(OD):
        w2[jj * L:(jj + 1) * L, :] = _spread(
            cv_t, lambda x: x, lambda y: y - V * jj, lambda x, y: x < N, (L, JB))
    l3[...] = _spread(cv, lambda x: _div(x, PC), lambda y: mod(y, N), lambda x, y: mod(x, PC) == _div(y, N), (GR, PC * N))
    l4[...] = _spread(co, lambda x: mod(x, O), lambda y: _div(y, 16) * PC + mod(y, PC),
                      lambda x, y: _div(x, O) == _div(mod(y, 16), PC), (4 * O, N * 4))

    pl.semaphore_wait(barrier, 3)

    def send(c, k):
        return pltpu.make_async_remote_copy(
            src_ref=g_send.at[c, k], dst_ref=g_recv.at[me, c], send_sem=send_sem.at[c, k],
            recv_sem=recv_sem.at[me, c], device_id=(f, peers[k]), device_id_type=MESH)

    def step_p(p, _):
        slot = lax.rem(p, SLOTS)
        a_copy(p, slot).wait()
        lhs = l1[...]
        for q in range(0, N, 4):
            x0 = jnp.pad(a_buf[slot, q:q + 2].reshape(2 * N, N), ((0, 0), (0, L - N)))
            x1 = jnp.pad(a_buf[slot, q + 2:q + 4].reshape(2 * N, N), ((0, 0), (0, L - N)))
            t = _dot(lhs, jnp.concatenate([x0, x1], axis=1))
            t_s[q * O:(q + 2) * O, :] = t[:, :L]
            t_s[(q + 2) * O:(q + 4) * O, :] = t[:, L:]

        @pl.when(p + SLOTS < NP)
        def _():
            a_copy(p + SLOTS, slot).start()

        pc = lax.rem(p, PC)
        rows = pl.ds(pl.multiple_of(pc * N, N), N)
        for d in range(NDEV):
            x = [t_s[pl.ds(d * OD + jj, N, stride=O), :].astype(BF16) for jj in range(OD)]
            h_s[d, rows, :256] = _dot(jnp.concatenate(x[:4], axis=1), w2[:4 * L, :256]).astype(BF16)
            h_s[d, rows, 256:] = _dot(jnp.concatenate(x[2:], axis=1), w2[2 * L:, 256:]).astype(BF16)

        @pl.when(pc == PC - 1)
        def _():
            c = p // PC
            for k in range(3):
                g_send[c, k] = _dot(l3[...], h_s[peers[k]]).astype(BF16)
                send(c, k).start()
            g_recv[me, c] = _dot(l3[...], h_s[me]).astype(BF16)
        return 0

    lax.fori_loop(0, NP, step_p, 0)

    ev = jnp.broadcast_to(ev_ref[...], (L, V))
    ev = jnp.pad(ev, ((0, 0), (0, L - V)))
    pair = ev + ev.T
    inside = (_rows((80, L)) < V) & (_cols((80, L)) < V)

    def recip(i, _):
        for jj in range(OD):
            den = (eo_ref[i] + eo_ref[me * OD + jj]) - pair[:80]
            r_s[i * OD + jj] = jnp.where(inside, 1.0 / den, 0.0)
        return 0

    lax.fori_loop(0, O, recip, 0)
    v_s[:, 4 * AQ * O:, :] = jnp.zeros((3, 4 * O, L), F32)

    for c in range(NC):
        for k in range(3):
            d = peers[k]
            pltpu.make_async_remote_copy(
                src_ref=g_send.at[c, k], dst_ref=g_recv.at[d, c], send_sem=send_sem.at[c, k],
                recv_sem=recv_sem.at[d, c], device_id=(f, d), device_id_type=MESH).wait()

    def contract(t, _):
        rows = pl.ds(pl.multiple_of(t * 16, 16), 16)
        g = g_recv[:, :, rows, :].reshape(NDEV * NC * 16, JB)
        v = _dot(l4[...], g)
        for n in range(3):
            v_s[n, pl.ds(pl.multiple_of(t * 4 * O, 4 * O), 4 * O), :] = v[:, n * L:(n + 1) * L]
        return 0

    lax.fori_loop(0, AQ, contract, 0)

    def energy(i, _):
        tiles = [v_s[t, pl.ds(i, 80, stride=O), :] for t in range(3)]
        lane = lax.broadcasted_iota(jnp.int32, (80, L), 1)
        for jj in range(OD):
            t, off = divmod(V * jj, L)
            m = pltpu.roll(tiles[t], (L - off) % L, axis=1) if off else tiles[t]
            if off + V > L:
                m = jnp.where(lane < L - off, m, pltpu.roll(tiles[t + 1], L - off, axis=1))
            mt = jnp.pad(m, ((0, L - 80), (0, 0))).T[:80]
            term = m * (2.0 * m - mt) * r_s[i * OD + jj]
            e_s[jj, pl.ds(pl.multiple_of(i * 8, 8), 8), :] = jnp.sum(term.reshape(10, 8, L), axis=0)
        return 0

    lax.fori_loop(0, O, energy, 0)
    for jj in range(OD):
        tot = e_s[jj, pl.ds(0, O, stride=8), :]
        for s in range(1, 8):
            tot = tot + e_s[jj, pl.ds(s, O, stride=8), :]
        col = jnp.sum(jnp.pad(tot, ((0, 32 - O), (0, 0))).T, axis=0, keepdims=True)
        out_ref[jj:jj + 1, :] = col[:, :O]


def solution(mesh):
    def per_device(a_ints, c_occ, c_vir, eps_occ, eps_vir):
        vm = pl.BlockSpec(memory_space=pltpu.VMEM)
        e = pl.pallas_call(
            kernel,
            out_shape=jax.ShapeDtypeStruct((OD, O), F32),
            in_specs=[pl.BlockSpec(memory_space=pl.ANY), vm, vm, pl.BlockSpec(memory_space=pltpu.SMEM), vm],
            out_specs=vm,
            scratch_shapes=[
                pltpu.VMEM((SLOTS, N, N, N), BF16),
                pltpu.VMEM((2 * O, 2 * N), BF16),
                pltpu.VMEM((OD * L, JB), BF16),
                pltpu.VMEM((GR, PC * N), BF16),
                pltpu.VMEM((4 * O, 4 * N), BF16),
                pltpu.VMEM((N * O, L), F32),
                pltpu.VMEM((NDEV, PC * N, JB), BF16),
                pltpu.VMEM((NC, 3, GR, JB), BF16),
                pltpu.VMEM((NDEV, NC, GR, JB), BF16),
                pltpu.VMEM((3, 80 * O, L), F32),
                pltpu.VMEM((O * OD, 80, L), F32),
                pltpu.VMEM((OD, O * 8, L), F32),
                pltpu.SemaphoreType.DMA((SLOTS,)),
                pltpu.SemaphoreType.DMA((NC, 3)),
                pltpu.SemaphoreType.DMA((NDEV, NC)),
            ],
            compiler_params=pltpu.CompilerParams(
                collective_id=0, has_side_effects=True, vmem_limit_bytes=60 * 2**20),
        )(a_ints, c_occ.T, c_vir.T, eps_occ, eps_vir.reshape(1, V))
        return e.T

    return jax.shard_map(
        per_device,
        mesh=mesh,
        in_specs=(P(("frag", "dev")), P("frag"), P("frag"), P("frag"), P("frag")),
        out_specs=P("frag", "dev"),
        check_vma=False,
    )
```

time: 204 us -> 80.5 us (0.39)
  waiting for transfers between devices: 103 us -> 0 us
  Pallas kernels: 0 us -> 79.1 us
  matrix products: 60.6 us -> 0 us
  local copies, waits for them, and re-layouts: 28.5 us -> 1.28 us
  starting transfers between devices: 6.12 us -> 0 us
  other arithmetic: 5.7 us -> 0 us
    all_to_all x1 -> x0, waiting for transfers between devices: 103 us -> none  [per_device(): half_mo = lax.all_to_all(half_mo, 'dev', 2, 0, tiled=True)]
    pallas_call x0 -> x1, Pallas kernels: none -> 79.1 us  [per_device(): pl.pallas_call(kernel, out_shape=jax.ShapeDtypeStruct((OD, O), F32), in_s...]
    dot_general x3 -> x0, matrix products: 60.6 us -> none  [the longest x1 25.6 us: per_device(): jnp.einsum('pqrs,rj->pqsj', a_ints, c_occ, preferred_element_type=jnp.flo...]
    convert_element_type x1 -> x0, local copies, waits for them, and re-layouts: 13.4 us -> none  [per_device(): jnp.einsum('pqsj,sb->pqjb', t_one, c_vir, preferred_element_type=jnp.floa...]
    all_to_all x1 -> x0, local copies, waits for them, and re-layouts: 8.76 us -> none  [per_device(): half_mo = lax.all_to_all(half_mo, 'dev', 2, 0, tiled=True)]
    dot_general x1 -> x0, local copies, waits for them, and re-layouts: 6.28 us -> none  [per_device(): jnp.einsum('pjba,pi->jbai', g_mat, c_occ, preferred_element_type=jnp.floa...]
    all_to_all x1 -> x0, starting transfers between devices: 6.12 us -> none  [per_device(): half_mo = lax.all_to_all(half_mo, 'dev', 2, 0, tiled=True)]
    reduce_sum x1 -> x0, other arithmetic: 5.54 us -> none  [pair_energies(): pair_ji = jnp.sum(v_mo * (2.0 * v_mo - v_swap) / denominator, axis=(1, 2))]
  transfers between devices with their start and end apart: 1 -> 0, of which waited for: 1 -> 0; matrix products, arithmetic and copies ran while one was open for 0% -> 0% of each run, Pallas kernels for 0% -> 0%
where the time goes in v1:
time: 80.5 us; the launch traced here: 80.4 us
  Pallas kernels  79.1 us (98%)
  local copies, waits for them, and re-layouts  1.28 us (2%)
    pallas_call x1, Pallas kernels, per_device(): pl.pallas_call(kernel, out_shape=jax.ShapeDtypeStruct((OD, O), F32), in_s...  79.1 us

profile of v1, /device:TPU:0, one launch (start us, length us, event | category | flops | bytes accessed | tf_op | source)
XLA Modules:
  0.0 80.4 jit_solution(15122453032700890579)
XLA Ops:
  0.0 79.1 %shard_map.55 = f32[5,20]{1,0:T(8,128)} custom-call(bf16[24,96,96,96]{3,2,1,0:T(8,128)(2,1)} %a_hbm.1, bf16[20,96]{1,0:T(8,128)(2,1)} %bitcast.6, bf16[75,96]{1,0:T(8,128)(2,1)} %bitcast.4, f32[20]{0:T(128)} %eo_ref.1, f32[1,75]{1,0:T(1,128)} %bitcast.7), custom_call_target="tpu_custom_call" | custom-call | tf_op jit(solution)/shard_map/pallas_call | solution.py:182
  79.1 1.3 %copy.7 = f32[20,5]{0,1:T(8,128)} copy(f32[20,5]{0,1:T(8,128)} %bitcast.5) | data formatting | bytes 800

commit v2 on v1

--- a/solution.py
+++ b/solution.py
@@ -22,7 +22,12 @@
 NC = NP // PC
 AQ = 19
 GR = AQ * 4 * PC
-SLOTS = 3
+SLOTS = 6
+T1 = 10
+GH = T1 * 16
+XR = GR - GH
+VQ = AQ - T1
+IG = O // 2
 
 
 def _dot(x, y):
@@ -53,8 +58,8 @@
     return jnp.where(keep(_rows(shape), _cols(shape)), full, 0.0).astype(BF16)
 
 
-def kernel(a_hbm, co_ref, cv_ref, eo_ref, ev_ref, out_ref, a_buf, l1, w2, l3, l4, t_s, h_s, g_send, g_recv,
-           v_s, r_s, e_s, a_sem, send_sem, recv_sem):
+def kernel(a_hbm, co_ref, cv_ref, eo_ref, ev_ref, out_ref, a_buf, l1, w2, l3, l4, t_s, h_s, g_send, g_own, g_near, g_far,
+           x_near, v_send, v_recv, v_s, r_s, e_s, a_sem, send_sem, far_sem, near_sem, x_sem, vs_sem, vr_sem):
     f, me = lax.axis_index("frag"), lax.axis_index("dev")
     chip, core = me // 2, lax.rem(me, 2)
     far0 = (1 - chip) * 2 + core
@@ -80,15 +85,34 @@
         w2[jj * L:(jj + 1) * L, :] = _spread(
             cv_t, lambda x: x, lambda y: y - V * jj, lambda x, y: x < N, (L, JB))
     l3[...] = _spread(cv, lambda x: _div(x, PC), lambda y: mod(y, N), lambda x, y: mod(x, PC) == _div(y, N), (GR, PC * N))
-    l4[...] = _spread(co, lambda x: mod(x, O), lambda y: _div(y, 16) * PC + mod(y, PC),
-                      lambda x, y: _div(x, O) == _div(mod(y, 16), PC), (4 * O, N * 4))
-
-    pl.semaphore_wait(barrier, 3)
-
-    def send(c, k):
-        return pltpu.make_async_remote_copy(
-            src_ref=g_send.at[c, k], dst_ref=g_recv.at[me, c], send_sem=send_sem.at[c, k],
-            recv_sem=recv_sem.at[me, c], device_id=(f, peers[k]), device_id_type=MESH)
+
+    def source_p(y):
+        slot = _div(y, N)
+        src = jnp.where(slot == 0, me, jnp.where(slot == 1, near, jnp.where(slot == 2, far0, far1))).astype(F32)
+        return src * NP + _div(mod(y, N), 16) * PC + mod(y, PC)
+
+    l4[...] = _spread(co, lambda x: _div(x, 8) * 2 + mod(x, 2), source_p,
+                      lambda x, y: _div(mod(x, 8), 2) == _div(mod(y, 16), PC), (4 * O, N * 4))
+
+    def g_copy(c, k):
+        return pltpu.make_async_remote_copy(
+            src_ref=g_send.at[c, k, pl.ds(0, GH)], dst_ref=g_far.at[k, c], send_sem=send_sem.at[c, k],
+            recv_sem=far_sem.at[k, c], device_id=(f, peers[k]), device_id_type=MESH)
+
+    def x_copy(c):
+        return pltpu.make_async_remote_copy(
+            src_ref=g_send.at[c, 1, pl.ds(GH, XR)], dst_ref=x_near.at[c], send_sem=send_sem.at[c, 2],
+            recv_sem=x_sem.at[c], device_id=(f, near), device_id_type=MESH)
+
+    def n_copy(c):
+        return pltpu.make_async_remote_copy(
+            src_ref=g_send.at[c, 2], dst_ref=g_near.at[c], send_sem=send_sem.at[c, 3],
+            recv_sem=near_sem.at[c], device_id=(f, near), device_id_type=MESH)
+
+    def v_copy(g):
+        return pltpu.make_async_remote_copy(
+            src_ref=v_send.at[g], dst_ref=v_recv.at[g], send_sem=vs_sem.at[g],
+            recv_sem=vr_sem.at[g], device_id=(f, far0), device_id_type=MESH)
 
     def step_p(p, _):
         slot = lax.rem(p, SLOTS)
@@ -112,16 +136,44 @@
             h_s[d, rows, :256] = _dot(jnp.concatenate(x[:4], axis=1), w2[:4 * L, :256]).astype(BF16)
             h_s[d, rows, 256:] = _dot(jnp.concatenate(x[2:], axis=1), w2[2 * L:, 256:]).astype(BF16)
 
+        @pl.when(p == PC - 1)
+        def _():
+            pl.semaphore_wait(barrier, 3)
+
         @pl.when(pc == PC - 1)
         def _():
             c = p // PC
-            for k in range(3):
-                g_send[c, k] = _dot(l3[...], h_s[peers[k]]).astype(BF16)
-                send(c, k).start()
-            g_recv[me, c] = _dot(l3[...], h_s[me]).astype(BF16)
+            g_send[c, 0] = _dot(l3[...], h_s[far0]).astype(BF16)
+            g_copy(c, 0).start()
+            g_send[c, 1] = _dot(l3[...], h_s[far1]).astype(BF16)
+            g_copy(c, 1).start()
+            x_copy(c).start()
+            g_send[c, 2] = _dot(l3[...], h_s[near]).astype(BF16)
+            n_copy(c).start()
+            g_own[c] = _dot(l3[...], h_s[me]).astype(BF16)
         return 0
 
     lax.fori_loop(0, NP, step_p, 0)
+
+    def quad(own, other, t):
+        rows = pl.ds(pl.multiple_of(t * 16, 16), 16)
+        orows = pl.ds(pl.multiple_of((t - (AQ - other.shape[1] // 16)) * 16, 16), 16)
+        return jnp.concatenate([own[:, rows].reshape(N, JB), other[:, orows].reshape(N, JB)], axis=0)
+
+    for c in range(NC):
+        x_copy(c).wait_recv()
+
+    def partial(t, _):
+        v = _dot(l4[:, :2 * N], quad(g_send.at[:, 0], x_near, t))
+        rows = pl.ds(pl.multiple_of((t - T1) * 8, 8), 8)
+        for g in range(IG):
+            for n in range(3):
+                v_send[g, n, rows, :] = v[g * 8:(g + 1) * 8, n * L:(n + 1) * L]
+        return 0
+
+    lax.fori_loop(T1, AQ, partial, 0)
+    for g in range(IG):
+        v_copy(g).start()
 
     ev = jnp.broadcast_to(ev_ref[...], (L, V))
     ev = jnp.pad(ev, ((0, 0), (0, L - V)))
@@ -135,45 +187,67 @@
         return 0
 
     lax.fori_loop(0, O, recip, 0)
-    v_s[:, 4 * AQ * O:, :] = jnp.zeros((3, 4 * O, L), F32)
-
-    for c in range(NC):
-        for k in range(3):
-            d = peers[k]
-            pltpu.make_async_remote_copy(
-                src_ref=g_send.at[c, k], dst_ref=g_recv.at[d, c], send_sem=send_sem.at[c, k],
-                recv_sem=recv_sem.at[d, c], device_id=(f, d), device_id_type=MESH).wait()
+
+    v_s[:, :, AQ * 8:, :] = jnp.zeros((IG, 3, 8, L), F32)
+    for c in range(NC):
+        n_copy(c).wait_recv()
 
     def contract(t, _):
+        v = _dot(l4[:, :2 * N], quad(g_own, g_near, t))
+        rows = pl.ds(pl.multiple_of(t * 8, 8), 8)
+        for g in range(IG):
+            for n in range(3):
+                v_s[g, n, rows, :] = v[g * 8:(g + 1) * 8, n * L:(n + 1) * L]
+        return 0
+
+    lax.fori_loop(0, AQ, contract, 0)
+    for c in range(NC):
+        for k in range(2):
+            g_copy(c, k).wait_recv()
+
+    def contract_far(t, _):
         rows = pl.ds(pl.multiple_of(t * 16, 16), 16)
-        g = g_recv[:, :, rows, :].reshape(NDEV * NC * 16, JB)
-        v = _dot(l4[...], g)
-        for n in range(3):
-            v_s[n, pl.ds(pl.multiple_of(t * 4 * O, 4 * O), 4 * O), :] = v[:, n * L:(n + 1) * L]
-        return 0
-
-    lax.fori_loop(0, AQ, contract, 0)
-
-    def energy(i, _):
-        tiles = [v_s[t, pl.ds(i, 80, stride=O), :] for t in range(3)]
+        v = _dot(l4[:, 2 * N:], g_far[:, :, rows].reshape(2 * N, JB))
+        rows = pl.ds(pl.multiple_of(t * 8, 8), 8)
+        for g in range(IG):
+            for n in range(3):
+                v_s[g, n, rows, :] += v[g * 8:(g + 1) * 8, n * L:(n + 1) * L]
+        return 0
+
+    lax.fori_loop(0, T1, contract_far, 0)
+
+    def energy(g, _):
+        v_copy(g).wait_recv()
+        v_s[g, :, T1 * 8:AQ * 8, :] += v_recv[g]
         lane = lax.broadcasted_iota(jnp.int32, (80, L), 1)
-        for jj in range(OD):
-            t, off = divmod(V * jj, L)
-            m = pltpu.roll(tiles[t], (L - off) % L, axis=1) if off else tiles[t]
-            if off + V > L:
-                m = jnp.where(lane < L - off, m, pltpu.roll(tiles[t + 1], L - off, axis=1))
-            mt = jnp.pad(m, ((0, L - 80), (0, 0))).T[:80]
-            term = m * (2.0 * m - mt) * r_s[i * OD + jj]
-            e_s[jj, pl.ds(pl.multiple_of(i * 8, 8), 8), :] = jnp.sum(term.reshape(10, 8, L), axis=0)
-        return 0
-
-    lax.fori_loop(0, O, energy, 0)
+        for ii in range(2):
+            i = g * 2 + ii
+            tiles = [v_s[g, n, pl.ds(ii, 80, stride=2), :] for n in range(3)]
+            for jj in range(OD):
+                t, off = divmod(V * jj, L)
+                m = pltpu.roll(tiles[t], (L - off) % L, axis=1) if off else tiles[t]
+                if off + V > L:
+                    m = jnp.where(lane < L - off, m, pltpu.roll(tiles[t + 1], L - off, axis=1))
+                mt = jnp.pad(m, ((0, L - 80), (0, 0))).T[:80]
+                term = m * (2.0 * m - mt) * r_s[i * OD + jj]
+                e_s[jj, pl.ds(pl.multiple_of(i * 8, 8), 8), :] = jnp.sum(term.reshape(10, 8, L), axis=0)
+        return 0
+
+    lax.fori_loop(0, IG, energy, 0)
     for jj in range(OD):
         tot = e_s[jj, pl.ds(0, O, stride=8), :]
         for s in range(1, 8):
             tot = tot + e_s[jj, pl.ds(s, O, stride=8), :]
         col = jnp.sum(jnp.pad(tot, ((0, 32 - O), (0, 0))).T, axis=0, keepdims=True)
         out_ref[jj:jj + 1, :] = col[:, :O]
+
+    for c in range(NC):
+        g_copy(c, 0).wait_send()
+        g_copy(c, 1).wait_send()
+        x_copy(c).wait_send()
+        n_copy(c).wait_send()
+    for g in range(IG):
+        v_copy(g).wait_send()
 
 
 def solution(mesh):
@@ -193,13 +267,22 @@
                 pltpu.VMEM((N * O, L), F32),
                 pltpu.VMEM((NDEV, PC * N, JB), BF16),
                 pltpu.VMEM((NC, 3, GR, JB), BF16),
-                pltpu.VMEM((NDEV, NC, GR, JB), BF16),
-                pltpu.VMEM((3, 80 * O, L), F32),
+                pltpu.VMEM((NC, GR, JB), BF16),
+                pltpu.VMEM((NC, GR, JB), BF16),
+                pltpu.VMEM((2, NC, GH, JB), BF16),
+                pltpu.VMEM((NC, XR, JB), BF16),
+                pltpu.VMEM((IG, 3, VQ * 8, L), F32),
+                pltpu.VMEM((IG, 3, VQ * 8, L), F32),
+                pltpu.VMEM((IG, 3, 160, L), F32),
                 pltpu.VMEM((O * OD, 80, L), F32),
                 pltpu.VMEM((OD, O * 8, L), F32),
                 pltpu.SemaphoreType.DMA((SLOTS,)),
-                pltpu.SemaphoreType.DMA((NC, 3)),
-                pltpu.SemaphoreType.DMA((NDEV, NC)),
+                pltpu.SemaphoreType.DMA((NC, 4)),
+                pltpu.SemaphoreType.DMA((2, NC)),
+                pltpu.SemaphoreType.DMA((NC,)),
+                pltpu.SemaphoreType.DMA((NC,)),
+                pltpu.SemaphoreType.DMA((IG,)),
+                pltpu.SemaphoreType.DMA((IG,)),
             ],
             compiler_params=pltpu.CompilerParams(
                 collective_id=0, has_side_effects=True, vmem_limit_bytes=60 * 2**20),

time: 80.5 us -> 69 us (0.86)
  Pallas kernels: 79.1 us -> 67.6 us
    pallas_call x1, Pallas kernels: 79.1 us -> 67.6 us  [per_device(): pl.pallas_call(kernel, out_shape=jax.ShapeDtypeStruct((OD, O), F32), in_s...]
where the time goes in v2:
time: 69 us; the launch traced here: 68.9 us
  Pallas kernels  67.6 us (98%)
  local copies, waits for them, and re-layouts  1.28 us (2%)
    pallas_call x1, Pallas kernels, per_device(): pl.pallas_call(kernel, out_shape=jax.ShapeDtypeStruct((OD, O), F32), in_s...  67.6 us

profile of v2, /device:TPU:0, one launch (start us, length us, event | category | flops | bytes accessed | tf_op | source)
XLA Modules:
  0.0 68.9 jit_solution(9697533231891073765)
XLA Ops:
  0.0 67.6 %shard_map.55 = f32[5,20]{1,0:T(8,128)} custom-call(bf16[24,96,96,96]{3,2,1,0:T(8,128)(2,1)} %a_hbm.1, bf16[20,96]{1,0:T(8,128)(2,1)} %bitcast.6, bf16[75,96]{1,0:T(8,128)(2,1)} %bitcast.4, f32[20]{0:T(128)} %eo_ref.1, f32[1,75]{1,0:T(1,128)} %bitcast.7), custom_call_target="tpu_custom_call" | custom-call | tf_op jit(solution)/shard_map/pallas_call | solution.py:256
  67.6 1.3 %copy.7 = f32[20,5]{0,1:T(8,128)} copy(f32[20,5]{0,1:T(8,128)} %bitcast.5) | data formatting | bytes 800

commit v3 on v2

v3 whole, which is shorter than its diff:
```python
import functools

import jax
import jax.numpy as jnp
from jax import lax
from jax.experimental import pallas as pl
from jax.experimental.pallas import tpu as pltpu
from jax.sharding import PartitionSpec as P

MESH = pl.DeviceIdType.MESH
F32, BF16 = jnp.float32, jnp.bfloat16

N = 96
O = 20
V = 75
NDEV = 4
NP = N // NDEV
OD = O // NDEV
L = 128
JB = 384
PC = 2
NC = NP // PC
AO = 10
GR = AO * 8 * PC
AV = 76
SLOTS = 6
U1 = 4
GH = U1 * 16
XR = GR - GH
VR = (AV - U1 * 8) * 2
IG = O // 2


def _dot(x, y):
    return jnp.dot(x, y, preferred_element_type=F32)


def _div(x, d):
    return jnp.floor((x + 0.5) * (1.0 / d))


def _rows(shape):
    return lax.broadcasted_iota(jnp.int32, shape, 0).astype(F32)


def _cols(shape):
    return lax.broadcasted_iota(jnp.int32, shape, 1).astype(F32)


def _onehot(cond):
    return jnp.where(cond, 1.0, 0.0).astype(BF16)


def _spread(m, row_of, col_of, keep, shape):
    r_shape, c_shape = (shape[0], m.shape[0]), (m.shape[1], shape[1])
    left = _onehot(row_of(_rows(r_shape)) == _cols(r_shape))
    right = _onehot(_rows(c_shape) == col_of(_cols(c_shape)))
    full = _dot(_dot(left, m).astype(BF16), right)
    return jnp.where(keep(_rows(shape), _cols(shape)), full, 0.0).astype(BF16)


def kernel(a_hbm, co_hbm, cv_hbm, eo_hbm, ev_hbm, out_ref, co_ref, cv_ref, eo_ref, ev_ref, a_buf, l1, w2, l3, l4, l4f,
           t0_s, t1_s, h_s, g_send, g_own, g_near, g_far, x_near, v_send, v_recv, v_s, r_s, e_s,
           a_sem, in_sem, send_sem, far_sem, near_sem, x_sem, vs_sem, vr_sem):
    f, me = lax.axis_index("frag"), lax.axis_index("dev")
    chip, core = me // 2, lax.rem(me, 2)
    far0 = (1 - chip) * 2 + core
    far1 = (1 - chip) * 2 + 1 - core
    near = chip * 2 + 1 - core
    peers = (far0, far1, near)

    def a_copy(p, slot):
        return pltpu.make_async_copy(a_hbm.at[p], a_buf.at[slot], a_sem.at[slot])

    barrier = pltpu.get_barrier_semaphore()
    for d in peers:
        pl.semaphore_signal(barrier, inc=1, device_id=(f, d), device_id_type=MESH)
    small = [pltpu.make_async_copy(x, y, in_sem.at[k]) for k, (x, y) in enumerate(
        [(co_hbm, co_ref), (cv_hbm, cv_ref), (eo_hbm, eo_ref), (ev_hbm, ev_ref)])]
    for cp in small[:2]:
        cp.start()
    a_copy(0, 0).start()
    for cp in small[:2]:
        cp.wait()
    for s in range(1, SLOTS):
        a_copy(s, s).start()
    for cp in small[2:]:
        cp.start()

    co, cv = co_ref[...], cv_ref[...]
    mod = lambda x, d: x - d * _div(x, d)
    co_pad = jnp.pad(co.astype(F32), ((0, O), (0, 256 - N)))
    l1[...] = (co_pad + pltpu.roll(pltpu.roll(co_pad, O, axis=0), N, axis=1)).astype(BF16)[:, :2 * N]
    cv_t = jnp.pad(cv.astype(F32), ((0, L - V), (0, L - N))).T
    cv_pad = jnp.pad(cv_t, ((0, 0), (0, JB - L)))
    for jj in range(OD):
        w2[jj * L:(jj + 1) * L, :] = (pltpu.roll(cv_pad, V * jj, axis=1) if jj else cv_pad).astype(BF16)
    l3[...] = _spread(cv, lambda x: _div(x, PC), lambda y: mod(y, N), lambda x, y: mod(x, PC) == _div(y, N), (GR, PC * N))

    def spread_co(slot0, slot1):
        return _spread(
            co, lambda x: _div(x, 16) * 2 + mod(x, 2),
            lambda y: jnp.where(y < NC * 16, slot0, slot1).astype(F32) * NP + _div(mod(y, NC * 16), 16) * PC + mod(y, PC),
            lambda x, y: _div(mod(x, 16), 2) == _div(mod(y, 16), PC), (8 * O, 2 * NC * 16))

    def g_copy(c, k):
        return pltpu.make_async_remote_copy(
            src_ref=g_send.at[c, k, pl.ds(0, GH)], dst_ref=g_far.at[k, c], send_sem=send_sem.at[c, k],
            recv_sem=far_sem.at[k, c], device_id=(f, peers[k]), device_id_type=MESH)

    def x_copy(c):
        return pltpu.make_async_remote_copy(
            src_ref=g_send.at[c, 1, pl.ds(GH, XR)], dst_ref=x_near.at[c], send_sem=send_sem.at[c, 2],
            recv_sem=x_sem.at[c], device_id=(f, near), device_id_type=MESH)

    def n_copy(c):
        return pltpu.make_async_remote_copy(
            src_ref=g_send.at[c, 2], dst_ref=g_near.at[c], send_sem=send_sem.at[c, 3],
            recv_sem=near_sem.at[c], device_id=(f, near), device_id_type=MESH)

    def v_copy(g):
        return pltpu.make_async_remote_copy(
            src_ref=v_send.at[g], dst_ref=v_recv.at[g], send_sem=vs_sem.at[g],
            recv_sem=vr_sem.at[g], device_id=(f, far0), device_id_type=MESH)

    def first_step(slot, buf, q):
        x0 = jnp.pad(a_buf[slot, q:q + 2].reshape(2 * N, N), ((0, 0), (0, L - N)))
        x1 = jnp.pad(a_buf[slot, q + 2:q + 4].reshape(2 * N, N), ((0, 0), (0, L - N)))
        t = _dot(l1[...], jnp.concatenate([x0, x1], axis=1))
        buf[q * O:(q + 2) * O, :] = t[:, :L]
        buf[(q + 2) * O:(q + 4) * O, :] = t[:, L:]

    def second_step(buf, row):
        x = [jnp.concatenate([buf[pl.ds(d * OD + jj, N, stride=O), :].astype(BF16) for d in range(NDEV)], axis=0)
             for jj in range(OD)]
        h0 = _dot(jnp.concatenate(x[:4], axis=1), w2[:4 * L, :256]).astype(BF16)
        h1 = _dot(jnp.concatenate(x[2:], axis=1), w2[2 * L:, 256:]).astype(BF16)
        for d in range(NDEV):
            h_s[d, row * N:(row + 1) * N, :256] = h0[d * N:(d + 1) * N]
            h_s[d, row * N:(row + 1) * N, 256:] = h1[d * N:(d + 1) * N]

    def third_step(d):
        return _dot(l3[...], h_s[d]).astype(BF16)

    def chunk(c, _):
        p = c * PC
        slot = lax.rem(p, SLOTS)
        a_copy(p, slot).wait()
        for q in range(0, N, 4):
            first_step(slot, t0_s, q)
        a_copy(p + 1, slot + 1).wait()
        for q in range(0, N, 4):
            first_step(slot + 1, t1_s, q)
            if q == 8:
                second_step(t0_s, 0)

        second_step(t1_s, 1)
        g_send[c, 0] = third_step(far0)
        g_send[c, 1] = third_step(far1)
        g_send[c, 2] = third_step(near)
        g_own[c] = third_step(me)

        @pl.when(c == 0)
        def _():
            pl.semaphore_wait(barrier, 3)

        x_copy(c).start()
        g_copy(c, 0).start()
        g_copy(c, 1).start()
        n_copy(c).start()

        @pl.when(p + SLOTS < NP)
        def _():
            a_copy(p + SLOTS, slot).start()
            a_copy(p + 1 + SLOTS, slot + 1).start()

        return 0

    lax.fori_loop(0, NC, chunk, 0)

    l4[...] = spread_co(me, near)

    def octet(own, other, t, t_other):
        rows = pl.ds(pl.multiple_of(t * 16, 16), 16)
        orows = pl.ds(pl.multiple_of(t_other * 16, 16), 16)
        return jnp.concatenate([own[:, rows].reshape(NC * 16, JB), other[:, orows].reshape(NC * 16, JB)], axis=0)

    for c in range(NC):
        x_copy(c).wait_recv()

    def partial(t):
        v = _dot(l4[...], octet(g_send.at[:, 0], x_near, t, t - U1))
        r = min(16, AV * 2 - t * 16)
        for g in range(IG):
            for n in range(3):
                v_send[g, n, (t - U1) * 16:(t - U1) * 16 + r, :] = v[g * 16:g * 16 + r, n * L:(n + 1) * L]

    for t in range(U1, AO):
        partial(t)
    for g in range(IG):
        v_copy(g).start()

    l4f[...] = spread_co(far0, far1)

    for cp in small[2:]:
        cp.wait()
    ev = jnp.broadcast_to(ev_ref[...], (L, V))
    ev = jnp.pad(ev, ((0, 0), (0, L - V)))
    pair = ev + ev.T
    inside = (_rows((80, L)) < V) & (_cols((80, L)) < V)

    def recip(i, _):
        for jj in range(OD):
            den = (eo_ref[i] + eo_ref[me * OD + jj]) - pair[:80]
            r_s[i * OD + jj] = jnp.where(inside, 1.0 / den, 0.0)
        return 0

    lax.fori_loop(0, O, recip, 0)

    for c in range(NC):
        n_copy(c).wait_recv()

    def contract(t, _):
        v = _dot(l4[...], octet(g_own, g_near, t, t))
        rows = pl.ds(pl.multiple_of(t * 16, 16), 16)
        for g in range(IG):
            for n in range(3):
                v_s[g, n, rows, :] = v[g * 16:(g + 1) * 16, n * L:(n + 1) * L]
        return 0

    lax.fori_loop(0, AO, contract, 0)
    for c in range(NC):
        for k in range(2):
            g_copy(c, k).wait_recv()

    def contract_far(t, _):
        v = _dot(l4f[...], octet(g_far.at[0], g_far.at[1], t, t))
        rows = pl.ds(pl.multiple_of(t * 16, 16), 16)
        for g in range(IG):
            for n in range(3):
                v_s[g, n, rows, :] += v[g * 16:(g + 1) * 16, n * L:(n + 1) * L]
        return 0

    lax.fori_loop(0, U1, contract_far, 0)

    def energy(g, _):
        v_copy(g).wait_recv()
        v_s[g, :, U1 * 16:AV * 2, :] += v_recv[g]
        lane = lax.broadcasted_iota(jnp.int32, (80, L), 1)
        for ii in range(2):
            i = g * 2 + ii
            tiles = [v_s[g, n, pl.ds(ii, 80, stride=2), :] for n in range(3)]
            for jj in range(OD):
                t, off = divmod(V * jj, L)
                m = pltpu.roll(tiles[t], (L - off) % L, axis=1) if off else tiles[t]
                if off + V > L:
                    m = jnp.where(lane < L - off, m, pltpu.roll(tiles[t + 1], L - off, axis=1))
                mt = jnp.pad(m, ((0, L - 80), (0, 0))).T[:80]
                term = m * (2.0 * m - mt) * r_s[i * OD + jj]
                e_s[jj, pl.ds(pl.multiple_of(i * 8, 8), 8), :] = jnp.sum(term.reshape(10, 8, L), axis=0)
        return 0

    lax.fori_loop(0, IG, energy, 0)
    for jj in range(OD):
        tot = e_s[jj, pl.ds(0, O, stride=8), :]
        for s in range(1, 8):
            tot = tot + e_s[jj, pl.ds(s, O, stride=8), :]
        col = jnp.sum(jnp.pad(tot, ((0, 32 - O), (0, 0))).T, axis=0, keepdims=True)
        out_ref[jj:jj + 1, :] = col[:, :O]

    for c in range(NC):
        g_copy(c, 0).wait_send()
        g_copy(c, 1).wait_send()
        x_copy(c).wait_send()
        n_copy(c).wait_send()
    for g in range(IG):
        v_copy(g).wait_send()


def solution(mesh):
    def per_device(a_ints, c_occ, c_vir, eps_occ, eps_vir):
        vm = pl.BlockSpec(memory_space=pltpu.VMEM)
        e = pl.pallas_call(
            kernel,
            out_shape=pltpu.VMEM((OD, O), F32),
            in_specs=[pl.BlockSpec(memory_space=pltpu.HBM)] * 5,
            out_specs=vm,
            scratch_shapes=[
                pltpu.VMEM((O, N), BF16),
                pltpu.VMEM((V, N), BF16),
                pltpu.SMEM((O,), F32),
                pltpu.VMEM((1, V), F32),
                pltpu.VMEM((SLOTS, N, N, N), BF16),
                pltpu.VMEM((2 * O, 2 * N), BF16),
                pltpu.VMEM((OD * L, JB), BF16),
                pltpu.VMEM((GR, PC * N), BF16),
                pltpu.VMEM((8 * O, 2 * NC * 16), BF16),
                pltpu.VMEM((8 * O, 2 * NC * 16), BF16),
                pltpu.VMEM((N * O, L), F32),
                pltpu.VMEM((N * O, L), F32),
                pltpu.VMEM((NDEV, PC * N, JB), BF16),
                pltpu.VMEM((NC, 3, GR, JB), BF16),
                pltpu.VMEM((NC, GR, JB), BF16),
                pltpu.VMEM((NC, GR, JB), BF16),
                pltpu.VMEM((2, NC, GH, JB), BF16),
                pltpu.VMEM((NC, XR, JB), BF16),
                pltpu.VMEM((IG, 3, VR, L), F32),
                pltpu.VMEM((IG, 3, VR, L), F32),
                pltpu.VMEM((IG, 3, AO * 16, L), F32),
                pltpu.VMEM((O * OD, 80, L), F32),
                pltpu.VMEM((OD, O * 8, L), F32),
                pltpu.SemaphoreType.DMA((SLOTS,)),
                pltpu.SemaphoreType.DMA((4,)),
                pltpu.SemaphoreType.DMA((NC, 4)),
                pltpu.SemaphoreType.DMA((2, NC)),
                pltpu.SemaphoreType.DMA((NC,)),
                pltpu.SemaphoreType.DMA((NC,)),
                pltpu.SemaphoreType.DMA((IG,)),
                pltpu.SemaphoreType.DMA((IG,)),
            ],
            compiler_params=pltpu.CompilerParams(
                collective_id=0, has_side_effects=True, vmem_limit_bytes=60 * 2**20),
        )(a_ints, c_occ.T, c_vir.T, eps_occ, eps_vir.reshape(1, V))
        return e.T

    return jax.shard_map(
        per_device,
        mesh=mesh,
        in_specs=(P(("frag", "dev")), P("frag"), P("frag"), P("frag"), P("frag")),
        out_specs=P("frag", "dev"),
        check_vma=False,
    )
```

time: 69 us -> 64.8 us (0.939)
  Pallas kernels: 67.6 us -> 64 us
    pallas_call x1, Pallas kernels: 67.6 us -> 64 us  [per_device(): pl.pallas_call(kernel, out_shape=pltpu.VMEM((OD, O), F32), in_specs=[pl.B...]
where the time goes in v3:
time: 64.8 us; the launch traced here: 64.6 us
  Pallas kernels  64 us (99%)
    pallas_call x1, Pallas kernels, per_device(): pl.pallas_call(kernel, out_shape=pltpu.VMEM((OD, O), F32), in_specs=[pl.B...  64 us

profile of v3, /device:TPU:0, one launch (start us, length us, event | category | flops | bytes accessed | tf_op | source)
XLA Modules:
  0.0 64.6 jit_solution(10276419693735320106)
XLA Ops:
  0.0 64.0 %shard_map.55 = f32[5,20]{1,0:T(8,128)S(1)} custom-call(bf16[24,96,96,96]{3,2,1,0:T(8,128)(2,1)} %a_hbm.1, bf16[20,96]{1,0:T(8,128)(2,1)} %bitcast.6, bf16[75,96]{1,0:T(8,128)(2,1)} %bitcast.5, f32[20]{0:T(128)} %eo_hbm.1, f32[1,75]{1,0:T(1,128)} %bitcast.7), custom_call_target="tpu_custom_call" | custom-call | tf_op jit(solution)/shard_map/pallas_call | solution.py:283
  64.0 0.6 copy.7

commit v4 on v3

--- a/solution.py
+++ b/solution.py
@@ -24,10 +24,15 @@
 GR = AO * 8 * PC
 AV = 76
 SLOTS = 6
-U1 = 4
-GH = U1 * 16
-XR = GR - GH
-VR = (AV - U1 * 8) * 2
+A1 = 28
+U0 = A1 // 8
+U2 = -(-A1 // 16)
+PH = U2 * 16
+XR = GR - U0 * 16
+VT = (V - A1) * 2
+VO = (A1 - U0 * 8) * 2
+VR = -(-VT // 8) * 8
+FK = NP * 16
 IG = O // 2
 
 
@@ -59,9 +64,9 @@
     return jnp.where(keep(_rows(shape), _cols(shape)), full, 0.0).astype(BF16)
 
 
-def kernel(a_hbm, co_hbm, cv_hbm, eo_hbm, ev_hbm, out_ref, co_ref, cv_ref, eo_ref, ev_ref, a_buf, l1, w2, l3, l4, l4f,
-           t0_s, t1_s, h_s, g_send, g_own, g_near, g_far, x_near, v_send, v_recv, v_s, r_s, e_s,
-           a_sem, in_sem, send_sem, far_sem, near_sem, x_sem, vs_sem, vr_sem):
+def kernel(a_hbm, co_hbm, cv_hbm, eo_hbm, ev_hbm, out_ref, co_ref, cv_ref, eo_ref, ev_ref, a_buf, l1, w2, l3, lp, l4, l4f,
+           t0_s, t1_s, h_s, g_send, g_own, g_near, p_send, p_far, x_near, v_send, v_recv, v_s, r_s, e_s,
+           a_sem, in_sem, send_sem, ps_sem, pf_sem, near_sem, x_sem, vs_sem, vr_sem):
     f, me = lax.axis_index("frag"), lax.axis_index("dev")
     chip, core = me // 2, lax.rem(me, 2)
     far0 = (1 - chip) * 2 + core
@@ -72,6 +77,8 @@
     def a_copy(p, slot):
         return pltpu.make_async_copy(a_hbm.at[p], a_buf.at[slot], a_sem.at[slot])
 
+    if PH > A1:
+        p_far[:, :, :, PH - 16:, :] = jnp.zeros((2, NP, 3, 16, L), BF16)
     barrier = pltpu.get_barrier_semaphore()
     for d in peers:
         pl.semaphore_signal(barrier, inc=1, device_id=(f, d), device_id_type=MESH)
@@ -95,7 +102,12 @@
     cv_pad = jnp.pad(cv_t, ((0, 0), (0, JB - L)))
     for jj in range(OD):
         w2[jj * L:(jj + 1) * L, :] = (pltpu.roll(cv_pad, V * jj, axis=1) if jj else cv_pad).astype(BF16)
-    l3[...] = _spread(cv, lambda x: _div(x, PC), lambda y: mod(y, N), lambda x, y: mod(x, PC) == _div(y, N), (GR, PC * N))
+    lp[...] = cv[:PH]
+
+    def build_l3():
+        twice = _dot(_onehot(_div(_rows((GR, V)), PC) == _cols((GR, V))), cv)
+        twice = jnp.pad(twice, ((0, 0), (0, 256 - N)))
+        l3[...] = jnp.where(mod(_rows((GR, 256)), PC) == 0, twice, pltpu.roll(twice, N, axis=1)).astype(BF16)[:, :PC * N]
 
     def spread_co(slot0, slot1):
         return _spread(
@@ -103,24 +115,24 @@
             lambda y: jnp.where(y < NC * 16, slot0, slot1).astype(F32) * NP + _div(mod(y, NC * 16), 16) * PC + mod(y, PC),
             lambda x, y: _div(mod(x, 16), 2) == _div(mod(y, 16), PC), (8 * O, 2 * NC * 16))
 
-    def g_copy(c, k):
+    def p_copy(p, k):
         return pltpu.make_async_remote_copy(
-            src_ref=g_send.at[c, k, pl.ds(0, GH)], dst_ref=g_far.at[k, c], send_sem=send_sem.at[c, k],
-            recv_sem=far_sem.at[k, c], device_id=(f, peers[k]), device_id_type=MESH)
+            src_ref=p_send.at[p, k, :, pl.ds(0, A1)], dst_ref=p_far.at[k, p, :, pl.ds(0, A1)], send_sem=ps_sem.at[p, k],
+            recv_sem=pf_sem.at[k, p], device_id=(f, peers[k]), device_id_type=MESH)
 
     def x_copy(c):
         return pltpu.make_async_remote_copy(
-            src_ref=g_send.at[c, 1, pl.ds(GH, XR)], dst_ref=x_near.at[c], send_sem=send_sem.at[c, 2],
+            src_ref=g_send.at[c, 1, pl.ds(U0 * 16, XR)], dst_ref=x_near.at[c], send_sem=send_sem.at[c, 0],
             recv_sem=x_sem.at[c], device_id=(f, near), device_id_type=MESH)
 
     def n_copy(c):
         return pltpu.make_async_remote_copy(
-            src_ref=g_send.at[c, 2], dst_ref=g_near.at[c], send_sem=send_sem.at[c, 3],
+            src_ref=g_send.at[c, 2], dst_ref=g_near.at[c], send_sem=send_sem.at[c, 1],
             recv_sem=near_sem.at[c], device_id=(f, near), device_id_type=MESH)
 
     def v_copy(g):
         return pltpu.make_async_remote_copy(
-            src_ref=v_send.at[g], dst_ref=v_recv.at[g], send_sem=vs_sem.at[g],
+            src_ref=v_send.at[g, :, pl.ds(0, VT)], dst_ref=v_recv.at[g, :, pl.ds(0, VT)], send_sem=vs_sem.at[g],
             recv_sem=vr_sem.at[g], device_id=(f, far0), device_id_type=MESH)
 
     def first_step(slot, buf, q):
@@ -139,44 +151,80 @@
             h_s[d, row * N:(row + 1) * N, :256] = h0[d * N:(d + 1) * N]
             h_s[d, row * N:(row + 1) * N, 256:] = h1[d * N:(d + 1) * N]
 
-    def third_step(d):
-        return _dot(l3[...], h_s[d]).astype(BF16)
+    def piece(p, row):
+        for k in range(2):
+            g = _dot(lp[...], h_s[peers[k], row * N:(row + 1) * N, :]).astype(BF16)
+            for n in range(3):
+                p_send[p, k, n] = g[:, n * L:(n + 1) * L]
+
+    def third_step(c, k):
+        r0 = U0 * 16 if k < 2 else 0
+        g = _dot(l3[r0:, :], h_s[(far0, far1, near, me)[k]]).astype(BF16)
+        if k < 3:
+            g_send[c, k, r0:, :] = g
+        else:
+            g_own[c] = g
+
+    def prefetch(p, slot):
+        @pl.when(p + SLOTS < NP)
+        def _():
+            a_copy(p + SLOTS, slot).start()
+            a_copy(p + 1 + SLOTS, slot + 1).start()
+
+    def send_piece(p):
+        p_copy(p, 0).start()
+        p_copy(p, 1).start()
+
+    a_copy(0, 0).wait()
+    for q in range(0, N, 4):
+        first_step(0, t0_s, q)
+    second_step(t0_s, 0)
+    piece(0, 0)
+    pl.semaphore_wait(barrier, 3)
+    send_piece(0)
+    a_copy(1, 1).wait()
+    for q in range(0, N, 4):
+        first_step(1, t1_s, q)
+    build_l3()
+    prefetch(0, 0)
 
     def chunk(c, _):
         p = c * PC
         slot = lax.rem(p, SLOTS)
         a_copy(p, slot).wait()
-        for q in range(0, N, 4):
+        for n, q in enumerate(range(0, N, 4)):
+            if n == 1:
+                second_step(t1_s, 1)
             first_step(slot, t0_s, q)
+            if n == 8:
+                piece(p - 1, 1)
+            if n in (11, 14, 17, 20):
+                third_step(c - 1, (n - 11) // 3)
+        send_piece(p - 1)
+        x_copy(c - 1).start()
+        n_copy(c - 1).start()
         a_copy(p + 1, slot + 1).wait()
-        for q in range(0, N, 4):
+        for n, q in enumerate(range(0, N, 4)):
+            if n == 1:
+                second_step(t0_s, 0)
             first_step(slot + 1, t1_s, q)
-            if q == 8:
-                second_step(t0_s, 0)
-
-        second_step(t1_s, 1)
-        g_send[c, 0] = third_step(far0)
-        g_send[c, 1] = third_step(far1)
-        g_send[c, 2] = third_step(near)
-        g_own[c] = third_step(me)
-
-        @pl.when(c == 0)
-        def _():
-            pl.semaphore_wait(barrier, 3)
-
-        x_copy(c).start()
-        g_copy(c, 0).start()
-        g_copy(c, 1).start()
-        n_copy(c).start()
-
-        @pl.when(p + SLOTS < NP)
-        def _():
-            a_copy(p + SLOTS, slot).start()
-            a_copy(p + 1 + SLOTS, slot + 1).start()
-
+            if n == 12:
+                piece(p, 0)
+        send_piece(p)
+        prefetch(p, slot)
         return 0
 
-    lax.fori_loop(0, NC, chunk, 0)
+    lax.fori_loop(1, NC, chunk, 0)
+    last = NC - 1
+    second_step(t1_s, 1)
+    third_step(last, 1)
+    third_step(last, 0)
+    piece(NP - 1, 1)
+    x_copy(last).start()
+    send_piece(NP - 1)
+    third_step(last, 2)
+    n_copy(last).start()
+    third_step(last, 3)
 
     l4[...] = spread_co(me, near)
 
@@ -189,18 +237,23 @@
         x_copy(c).wait_recv()
 
     def partial(t):
-        v = _dot(l4[...], octet(g_send.at[:, 0], x_near, t, t - U1))
-        r = min(16, AV * 2 - t * 16)
+        v = _dot(l4[...], octet(g_send.at[:, 0], x_near, t, t - U0))
+        r0 = VO if t == U0 else 0
+        r1 = min(16, V * 2 - t * 16)
+        at = t * 16 - A1 * 2
         for g in range(IG):
             for n in range(3):
-                v_send[g, n, (t - U1) * 16:(t - U1) * 16 + r, :] = v[g * 16:g * 16 + r, n * L:(n + 1) * L]
-
-    for t in range(U1, AO):
+                v_send[g, n, at + r0:at + r1, :] = v[g * 16 + r0:g * 16 + r1, n * L:(n + 1) * L]
+
+    for t in range(U0, AO):
         partial(t)
     for g in range(IG):
         v_copy(g).start()
 
-    l4f[...] = spread_co(far0, far1)
+    l4f[...] = _spread(
+        co, lambda x: _div(x, 32) * 2 + mod(x, 2),
+        lambda y: jnp.where(y < FK, far0, far1).astype(F32) * NP + _div(mod(y, FK), 16),
+        lambda x, y: _div(mod(x, 32), 2) == mod(y, 16), (16 * O, 2 * FK))
 
     for cp in small[2:]:
         cp.wait()
@@ -229,23 +282,19 @@
         return 0
 
     lax.fori_loop(0, AO, contract, 0)
-    for c in range(NC):
+    for p in range(NP):
         for k in range(2):
-            g_copy(c, k).wait_recv()
-
-    def contract_far(t, _):
-        v = _dot(l4f[...], octet(g_far.at[0], g_far.at[1], t, t))
-        rows = pl.ds(pl.multiple_of(t * 16, 16), 16)
-        for g in range(IG):
-            for n in range(3):
-                v_s[g, n, rows, :] += v[g * 16:(g + 1) * 16, n * L:(n + 1) * L]
-        return 0
-
-    lax.fori_loop(0, U1, contract_far, 0)
+            p_copy(p, k).wait_recv()
+
+    for u in range(U2):
+        for n in range(3):
+            v = _dot(l4f[...], p_far[:, :, n, u * 16:(u + 1) * 16, :].reshape(2 * FK, L))
+            for g in range(IG):
+                v_s[g, n, u * 32:(u + 1) * 32, :] += v[g * 32:(g + 1) * 32]
 
     def energy(g, _):
         v_copy(g).wait_recv()
-        v_s[g, :, U1 * 16:AV * 2, :] += v_recv[g]
+        v_s[g, :, A1 * 2:V * 2, :] += v_recv[g, :, :VT]
         lane = lax.broadcasted_iota(jnp.int32, (80, L), 1)
         for ii in range(2):
             i = g * 2 + ii
@@ -268,9 +317,10 @@
         col = jnp.sum(jnp.pad(tot, ((0, 32 - O), (0, 0))).T, axis=0, keepdims=True)
         out_ref[jj:jj + 1, :] = col[:, :O]
 
+    for p in range(NP):
+        p_copy(p, 0).wait_send()
+        p_copy(p, 1).wait_send()
     for c in range(NC):
-        g_copy(c, 0).wait_send()
-        g_copy(c, 1).wait_send()
         x_copy(c).wait_send()
         n_copy(c).wait_send()
     for g in range(IG):
@@ -294,15 +344,17 @@
                 pltpu.VMEM((2 * O, 2 * N), BF16),
                 pltpu.VMEM((OD * L, JB), BF16),
                 pltpu.VMEM((GR, PC * N), BF16),
+                pltpu.VMEM((PH, N), BF16),
                 pltpu.VMEM((8 * O, 2 * NC * 16), BF16),
-                pltpu.VMEM((8 * O, 2 * NC * 16), BF16),
+                pltpu.VMEM((16 * O, 2 * FK), BF16),
                 pltpu.VMEM((N * O, L), F32),
                 pltpu.VMEM((N * O, L), F32),
                 pltpu.VMEM((NDEV, PC * N, JB), BF16),
                 pltpu.VMEM((NC, 3, GR, JB), BF16),
                 pltpu.VMEM((NC, GR, JB), BF16),
                 pltpu.VMEM((NC, GR, JB), BF16),
-                pltpu.VMEM((2, NC, GH, JB), BF16),
+                pltpu.VMEM((NP, 2, 3, PH, L), BF16),
+                pltpu.VMEM((2, NP, 3, PH, L), BF16),
                 pltpu.VMEM((NC, XR, JB), BF16),
                 pltpu.VMEM((IG, 3, VR, L), F32),
                 pltpu.VMEM((IG, 3, VR, L), F32),
@@ -311,8 +363,9 @@
                 pltpu.VMEM((OD, O * 8, L), F32),
                 pltpu.SemaphoreType.DMA((SLOTS,)),
                 pltpu.SemaphoreType.DMA((4,)),
-                pltpu.SemaphoreType.DMA((NC, 4)),
-                pltpu.SemaphoreType.DMA((2, NC)),
+                pltpu.SemaphoreType.DMA((NC, 2)),
+                pltpu.SemaphoreType.DMA((NP, 2)),
+                pltpu.SemaphoreType.DMA((2, NP)),
                 pltpu.SemaphoreType.DMA((NC,)),
                 pltpu.SemaphoreType.DMA((NC,)),
                 pltpu.SemaphoreType.DMA((IG,)),

time: 64.8 us -> 63.8 us (0.985)
  Pallas kernels: 64 us -> 63.1 us
    pallas_call x1, Pallas kernels: 64 us -> 63.1 us  [per_device(): pl.pallas_call(kernel, out_shape=pltpu.VMEM((OD, O), F32), in_specs=[pl.B...]
where the time goes in v4:
time: 63.8 us; the launch traced here: 63.7 us
  Pallas kernels  63.1 us (99%)
    pallas_call x1, Pallas kernels, per_device(): pl.pallas_call(kernel, out_shape=pltpu.VMEM((OD, O), F32), in_specs=[pl.B...  63.1 us

profile of v4, /device:TPU:0, one launch (start us, length us, event | category | flops | bytes accessed | tf_op | source)
XLA Modules:
  0.0 63.7 jit_solution(16325752061083178686)
XLA Ops:
  0.0 63.1 %shard_map.55 = f32[5,20]{1,0:T(8,128)S(1)} custom-call(bf16[24,96,96,96]{3,2,1,0:T(8,128)(2,1)} %a_hbm.1, bf16[20,96]{1,0:T(8,128)(2,1)} %bitcast.6, bf16[75,96]{1,0:T(8,128)(2,1)} %bitcast.5, f32[20]{0:T(128)} %eo_hbm.1, f32[1,75]{1,0:T(1,128)} %bitcast.7), custom_call_target="tpu_custom_call" | custom-call | tf_op jit(solution)/shard_map/pallas_call | solution.py:333
  63.1 0.6 copy.7

commit v5 on v4

--- a/solution.py
+++ b/solution.py
@@ -24,7 +24,7 @@
 GR = AO * 8 * PC
 AV = 76
 SLOTS = 6
-A1 = 28
+A1 = 26
 U0 = A1 // 8
 U2 = -(-A1 // 16)
 PH = U2 * 16
@@ -77,16 +77,16 @@
     def a_copy(p, slot):
         return pltpu.make_async_copy(a_hbm.at[p], a_buf.at[slot], a_sem.at[slot])
 
+    small = [pltpu.make_async_copy(x, y, in_sem.at[k]) for k, (x, y) in enumerate(
+        [(co_hbm, co_ref), (cv_hbm, cv_ref), (eo_hbm, eo_ref), (ev_hbm, ev_ref)])]
+    for cp in small[:2]:
+        cp.start()
+    a_copy(0, 0).start()
     if PH > A1:
         p_far[:, :, :, PH - 16:, :] = jnp.zeros((2, NP, 3, 16, L), BF16)
     barrier = pltpu.get_barrier_semaphore()
     for d in peers:
         pl.semaphore_signal(barrier, inc=1, device_id=(f, d), device_id_type=MESH)
-    small = [pltpu.make_async_copy(x, y, in_sem.at[k]) for k, (x, y) in enumerate(
-        [(co_hbm, co_ref), (cv_hbm, cv_ref), (eo_hbm, eo_ref), (ev_hbm, ev_ref)])]
-    for cp in small[:2]:
-        cp.start()
-    a_copy(0, 0).start()
     for cp in small[:2]:
         cp.wait()
     for s in range(1, SLOTS):
@@ -200,9 +200,8 @@
                 piece(p - 1, 1)
             if n in (11, 14, 17, 20):
                 third_step(c - 1, (n - 11) // 3)
+        x_copy(c - 1).start()
         send_piece(p - 1)
-        x_copy(c - 1).start()
-        n_copy(c - 1).start()
         a_copy(p + 1, slot + 1).wait()
         for n, q in enumerate(range(0, N, 4)):
             if n == 1:
@@ -218,12 +217,11 @@
     last = NC - 1
     second_step(t1_s, 1)
     third_step(last, 1)
+    x_copy(last).start()
     third_step(last, 0)
     piece(NP - 1, 1)
-    x_copy(last).start()
     send_piece(NP - 1)
     third_step(last, 2)
-    n_copy(last).start()
     third_step(last, 3)
 
     l4[...] = spread_co(me, near)
@@ -249,6 +247,8 @@
         partial(t)
     for g in range(IG):
         v_copy(g).start()
+    for c in range(NC):
+        n_copy(c).start()
 
     l4f[...] = _spread(
         co, lambda x: _div(x, 32) * 2 + mod(x, 2),
@@ -292,8 +292,14 @@
             for g in range(IG):
                 v_s[g, n, u * 32:(u + 1) * 32, :] += v[g * 32:(g + 1) * 32]
 
+    for p in range(NP):
+        p_copy(p, 0).wait_send()
+        p_copy(p, 1).wait_send()
+    for c in range(NC):
+        x_copy(c).wait_send()
+        n_copy(c).wait_send()
     def energy(g, _):
-        v_copy(g).wait_recv()
+        v_copy(g).wait()
         v_s[g, :, A1 * 2:V * 2, :] += v_recv[g, :, :VT]
         lane = lax.broadcasted_iota(jnp.int32, (80, L), 1)
         for ii in range(2):
@@ -316,15 +322,6 @@
             tot = tot + e_s[jj, pl.ds(s, O, stride=8), :]
         col = jnp.sum(jnp.pad(tot, ((0, 32 - O), (0, 0))).T, axis=0, keepdims=True)
         out_ref[jj:jj + 1, :] = col[:, :O]
-
-    for p in range(NP):
-        p_copy(p, 0).wait_send()
-        p_copy(p, 1).wait_send()
-    for c in range(NC):
-        x_copy(c).wait_send()
-        n_copy(c).wait_send()
-    for g in range(IG):
-        v_copy(g).wait_send()
 
 
 def solution(mesh):

time: 63.8 us -> 63.5 us (level)
  no operation moved by 1% of the time
where the time goes in v5:
time: 63.5 us; the launch traced here: 63.4 us
  Pallas kernels  62.8 us (99%)
    pallas_call x1, Pallas kernels, per_device(): pl.pallas_call(kernel, out_shape=pltpu.VMEM((OD, O), F32), in_specs=[pl.B...  62.8 us

profile of v5, /device:TPU:0, one launch (start us, length us, event | category | flops | bytes accessed | tf_op | source)
XLA Modules:
  0.0 63.4 jit_solution(16149382347045377918)
XLA Ops:
  0.0 62.8 %shard_map.55 = f32[5,20]{1,0:T(8,128)S(1)} custom-call(bf16[24,96,96,96]{3,2,1,0:T(8,128)(2,1)} %a_hbm.1, bf16[20,96]{1,0:T(8,128)(2,1)} %bitcast.6, bf16[75,96]{1,0:T(8,128)(2,1)} %bitcast.5, f32[20]{0:T(128)} %eo_hbm.1, f32[1,75]{1,0:T(1,128)} %bitcast.7), custom_call_target="tpu_custom_call" | custom-call | tf_op jit(solution)/shard_map/pallas_call | solution.py:330
  62.8 0.6 copy.7

commit v6 on v5

--- a/solution.py
+++ b/solution.py
@@ -82,6 +82,7 @@
     for cp in small[:2]:
         cp.start()
     a_copy(0, 0).start()
+    a_copy(1, 1).start()
     if PH > A1:
         p_far[:, :, :, PH - 16:, :] = jnp.zeros((2, NP, 3, 16, L), BF16)
     barrier = pltpu.get_barrier_semaphore()
@@ -89,7 +90,7 @@
         pl.semaphore_signal(barrier, inc=1, device_id=(f, d), device_id_type=MESH)
     for cp in small[:2]:
         cp.wait()
-    for s in range(1, SLOTS):
+    for s in range(2, SLOTS):
         a_copy(s, s).start()
     for cp in small[2:]:
         cp.start()
@@ -234,19 +235,21 @@
     for c in range(NC):
         x_copy(c).wait_recv()
 
-    def partial(t):
-        v = _dot(l4[...], octet(g_send.at[:, 0], x_near, t, t - U0))
+    def partial(t, g0, g1):
+        v = _dot(l4[g0 * 16:g1 * 16, :], octet(g_send.at[:, 0], x_near, t, t - U0))
         r0 = VO if t == U0 else 0
         r1 = min(16, V * 2 - t * 16)
         at = t * 16 - A1 * 2
-        for g in range(IG):
+        for g in range(g0, g1):
+            row = (g - g0) * 16
             for n in range(3):
-                v_send[g, n, at + r0:at + r1, :] = v[g * 16 + r0:g * 16 + r1, n * L:(n + 1) * L]
-
-    for t in range(U0, AO):
-        partial(t)
-    for g in range(IG):
-        v_copy(g).start()
+                v_send[g, n, at + r0:at + r1, :] = v[row + r0:row + r1, n * L:(n + 1) * L]
+
+    for g0, g1 in ((0, 3), (3, IG)):
+        for t in range(U0, AO):
+            partial(t, g0, g1)
+        for g in range(g0, g1):
+            v_copy(g).start()
     for c in range(NC):
         n_copy(c).start()
 

time: 63.5 us -> 63.4 us (level)
  no operation moved by 1% of the time
where the time goes in v6:
time: 63.4 us; the launch traced here: 63.3 us
  Pallas kernels  62.7 us (99%)
    pallas_call x1, Pallas kernels, per_device(): pl.pallas_call(kernel, out_shape=pltpu.VMEM((OD, O), F32), in_specs=[pl.B...  62.7 us

profile of v6, /device:TPU:0, one launch (start us, length us, event | category | flops | bytes accessed | tf_op | source)
XLA Modules:
  0.0 63.3 jit_solution(8321953232226376525)
XLA Ops:
  0.0 62.7 %shard_map.55 = f32[5,20]{1,0:T(8,128)S(1)} custom-call(bf16[24,96,96,96]{3,2,1,0:T(8,128)(2,1)} %a_hbm.1, bf16[20,96]{1,0:T(8,128)(2,1)} %bitcast.6, bf16[75,96]{1,0:T(8,128)(2,1)} %bitcast.5, f32[20]{0:T(128)} %eo_hbm.1, f32[1,75]{1,0:T(1,128)} %bitcast.7), custom_call_target="tpu_custom_call" | custom-call | tf_op jit(solution)/shard_map/pallas_call | solution.py:333
  62.7 0.6 copy.7
